TPU v7x, 32 devices: a whole 2x2x4 slice. The times are simulated.
32 devices in a mesh: grp: 4 (over y, x), dev: 8 (over z, core).
Axes of the slice: x: 2, y: 2, z: 4, core: 2. Of those that a mesh axis runs over, the one named last changes fastest.
Arguments:
- leaf_emit: float32 [3, 4096], P(None, 'dev'), may hold values from 0 to 1
- leaf_albedo: float32 [3, 4096], P(None, 'dev'), may hold values from 0.2 to 0.9
- leaf_radiosity: float32 [3, 4096], P(None, 'dev'), may hold values from 0.05 to 4
- leaf_area: float32 [4096], P('dev'), may hold values from 0.002 to 0.03
- parent_index: int32 [4096], P('dev'), may hold values from 0 to 255, as said below
- node_position: float32 [3, 6144], P(None, 'dev'), may hold values from -1 to 1
- node_angles: float32 [2, 6144], P(None, 'dev'), may hold values from -3.140625 to 3.140625
- block_receiver: int32 [4, 1024], P('grp', 'dev'), may hold values from 0 to 5
- block_source: int32 [4, 1024], P('grp', 'dev'), may hold values from 0 to 15
- block_count: int32 [4, 8], P('grp', 'dev'), may hold values from 16 to 128, as said below
Outputs:
- new_radiosity: float32 [3, 4096], P(None, 'dev')
Inputs may be any that keep to these rules, and one draw needn't show every extreme that they name: `parent_index`: within each shard's 512 leaves every cluster 0 to 255 is named at least once. The first block_count slots of a device are live, the rest are ignored. For every index of dev exactly one index of grp has 128 live slots; the others have at most 64.
All inputs are finite; a program needn't handle non-finite values.
Results may differ from a plain program's by a relative error of at most 0.0001.
Values sent between devices are 32-bit elements; how exact they have to be, the bound alone decides.
A program may use at most 64 MiB of HBM per device.

v0:
```python
import jax
import jax.numpy as jnp
from jax import lax
from jax.sharding import PartitionSpec as P

TILE = 128
batch_slots = 16


def unit_normals(node_angles):
    azimuth = node_angles[0]
    elevation = node_angles[1]
    return jnp.stack(
        [
            jnp.cos(azimuth) * jnp.cos(elevation),
            jnp.sin(azimuth) * jnp.cos(elevation),
            jnp.sin(elevation),
        ]
    )


def tile_irradiance(receivers, sources):
    offsets = [
        sources[axis_id][:, None, :] - receivers[axis_id][:, :, None] for axis_id in range(3)
    ]
    distance_sq = offsets[0] * offsets[0] + offsets[1] * offsets[1] + offsets[2] * offsets[2]
    facing_receiver = (
        receivers[3][:, :, None] * offsets[0]
        + receivers[4][:, :, None] * offsets[1]
        + receivers[5][:, :, None] * offsets[2]
    )
    facing_source = (
        sources[3][:, None, :] * offsets[0]
        + sources[4][:, None, :] * offsets[1]
        + sources[5][:, None, :] * offsets[2]
    )
    source_area = sources[6][:, None, :]
    factor = (
        source_area
        * jnp.maximum(facing_receiver, 0.0)
        * jnp.maximum(-facing_source, 0.0)
        / ((distance_sq + source_area) * (jnp.pi * distance_sq + source_area))
    )
    return jnp.einsum("bij,cbj->bci", factor, sources[7:10], precision=lax.Precision.HIGHEST)


def body(
    leaf_emit,
    leaf_albedo,
    leaf_radiosity,
    leaf_area,
    parent_index,
    node_position,
    node_angles,
    block_receiver,
    block_source,
    block_count,
):
    leaf_count = leaf_area.shape[0]
    node_count = node_position.shape[1]
    cluster_count = node_count - leaf_count
    tile_count = node_count // TILE
    slot_count = block_receiver.shape[1]
    normals = unit_normals(node_angles)
    parent_onehot = (
        parent_index[:, None] == jnp.arange(cluster_count, dtype=jnp.int32)[None, :]
    ).astype(jnp.float32)
    cluster_area = jnp.dot(leaf_area, parent_onehot, precision=lax.Precision.HIGHEST)
    weighted = jnp.dot(
        leaf_radiosity * leaf_area[None, :], parent_onehot, precision=lax.Precision.HIGHEST
    )
    cluster_radiosity = weighted / cluster_area[None, :]
    source_pack = jnp.concatenate(
        [
            node_position[:, leaf_count:],
            normals[:, leaf_count:],
            cluster_area[None, :],
            cluster_radiosity,
        ],
        axis=0,
    )
    receiver_pack = jnp.concatenate([node_position, normals], axis=0)
    linked = lax.all_to_all(receiver_pack, "dev", split_axis=1, concat_axis=1, tiled=True)
    receiver_tiles = linked.reshape(6, tile_count, TILE)
    everything = lax.all_gather(source_pack, "dev", axis=1, tiled=True)
    source_tiles = everything.reshape(10, -1, TILE)
    receiver_ids = block_receiver[0]
    source_ids = block_source[0]
    live_count = block_count[0, 0]
    step_slots = min(batch_slots, slot_count)

    def add_batch(rounds, totals):
        first = rounds * step_slots
        batch_receivers = lax.dynamic_slice_in_dim(receiver_ids, first, step_slots, 0)
        batch_sources = lax.dynamic_slice_in_dim(source_ids, first, step_slots, 0)
        batch_weight = (first + jnp.arange(step_slots, dtype=jnp.int32) < live_count).astype(
            jnp.float32
        )
        receivers = jnp.take(receiver_tiles, batch_receivers, axis=1)
        sources = jnp.take(source_tiles, batch_sources, axis=1)
        contrib = tile_irradiance(receivers, sources) * batch_weight[:, None, None]
        placement = (
            batch_receivers[:, None] == jnp.arange(tile_count, dtype=jnp.int32)[None, :]
        ).astype(jnp.float32)
        return totals + jnp.einsum(
            "bt,bci->cti", placement, contrib, precision=lax.Precision.HIGHEST
        )

    batch_total = (live_count + step_slots - 1) // step_slots
    totals = lax.fori_loop(0, batch_total, add_batch, jnp.zeros((3, tile_count, TILE), jnp.float32))
    partial_value = totals.reshape(3, node_count)
    summed = lax.psum(partial_value, "grp")
    irradiance = lax.all_to_all(summed, "dev", split_axis=1, concat_axis=1, tiled=True)
    pushed = jnp.dot(irradiance[:, leaf_count:], parent_onehot.T, precision=lax.Precision.HIGHEST)
    gathered = irradiance[:, :leaf_count] + pushed
    return leaf_emit + leaf_albedo * gathered


def solution(mesh):
    in_specs = (
        P(None, "dev"),
        P(None, "dev"),
        P(None, "dev"),
        P("dev"),
        P("dev"),
        P(None, "dev"),
        P(None, "dev"),
        P("grp", "dev"),
        P("grp", "dev"),
        P("grp", "dev"),
    )
    out_specs = P(None, "dev")
    return jax.shard_map(body, mesh=mesh, in_specs=in_specs, out_specs=out_specs, check_vma=False)
```

profile of v0, /device:TPU:0, one launch (start us, length us, event | category | flops | bytes accessed | tf_op | source)
XLA Modules:
  0.0 103.0 jit_solution(1958860069309156690)
XLA Ops:
  0.0 0.8 concatenate.17
  0.8 0.2 fusion.52
  1.2 0.6 copy.24
  1.9 6.4 %all-to-all-start = ((f32[6,8,96]{2,0,1:T(8,128)}), f32[6,8,96]{2,0,1:T(8,128)S(1)}, u32[]{:S(2)}, u32[]{:S(2)}) async-start(f32[6,8,96]{2,0,1:T(8,128)} %copy.24), calls=%async_computation | async-start | bytes 65536 | tf_op jit(solution)/shard_map/all_to_all | solution.py:83
  8.9 0.7 copy-done.7
  9.6 0.3 fusion.42
  9.9 0.4 copy-done.3
  10.3 0.3 convolution_divide_fusion
  10.6 0.7 slice-done
  11.3 14.5 %all_gather.3 = f32[10,2048]{1,0:T(8,128)S(1)} all-gather(f32[10,256]{1,0:T(8,128)S(1)} %fusion.48), channel_id=1, replica_groups=mesh['grp'=4,'dev'=8] {'dev'}, dimensions={1}, use_global_device_ids=true | all-gather | bytes 92160 | tf_op jit(solution)/shard_map/all_gather | solution.py:85
  26.1 0.6 copy-done
  26.7 12.4 %while.10 = (s32[]{:T(128)}, f32[3,6,128]{2,1,0:T(8,128)S(1)}, s32[]{:T(128)}, s32[128]{0:T(128)S(1)}, f32[10,16,128]{2,0,1:T(8,128)S(1)}, /*index=5*/s32[128]{0...) while((s32[]{:T(128)}, f32[3,6,128]{2,1,0:T(8,128)S(1)}, ...), condition=%wide.region_1.2_spmd, body=%wide.region_0.1_spmd.sunk | while | flops 17263236 | bytes 953843 | solution.py:110
  26.7 0.7 compare_and_fusion.5
  27.5 0.1 compare_and_fusion.4
  27.6 0.6 gather_fusion.1
  28.1 0.1 select_bitcast_fusion.5
  28.3 0.6 gather_fusion
  28.8 0.1 select_bitcast_fusion.4
  29.0 3.8 %convolution_multiply_fusion.2 = f32[16,3,128]{2,1,0:T(4,128)S(1)} fusion(f32[16,128]{1,0:T(8,128)S(1)} %bitcast.71, f32[16,128]{1,0:T(8,128)S(1)} %bitcast.72, f32[16,128]{1,0:T(8,128)S(1)} %bitcast.73, f32[16,128]{1,0:T(8,128)S(1)} %bitcast.78, f32[16,128]{1,0:T(8,128)S(1)} %bitcast.74, f32[16,128]{1,0:T(8,128)S(1)} %bitcast.79, ...), kind=kOutput, calls=%fused_computation.11.clone.1 | convolution fusion | flops 16783360 | bytes 164352 | tf_op jit(solution)/shard_map/while/body/bij,cbj->bci/dot_general | solution.py:44
  32.8 0.1 fusion.71
  32.9 0.7 compare_and_fusion.5
  33.7 0.6 gather_fusion.1
  34.3 0.1 select_bitcast_fusion.5
  34.5 0.6 gather_fusion
  35.0 0.1 select_bitcast_fusion.4
  35.2 3.8 %convolution_multiply_fusion.2 = f32[16,3,128]{2,1,0:T(4,128)S(1)} fusion(f32[16,128]{1,0:T(8,128)S(1)} %bitcast.71, f32[16,128]{1,0:T(8,128)S(1)} %bitcast.72, f32[16,128]{1,0:T(8,128)S(1)} %bitcast.73, f32[16,128]{1,0:T(8,128)S(1)} %bitcast.78, f32[16,128]{1,0:T(8,128)S(1)} %bitcast.74, f32[16,128]{1,0:T(8,128)S(1)} %bitcast.79, ...), kind=kOutput, calls=%fused_computation.11.clone.1 | convolution fusion | flops 16783360 | bytes 164352 | tf_op jit(solution)/shard_map/while/body/bij,cbj->bci/dot_general | solution.py:44
  38.9 0.1 fusion.71
  39.2 50.9 %psum.7 = f32[3,8,96]{2,1,0:T(8,128)S(1)} all-reduce(f32[3,8,96]{2,1,0:T(8,128)S(1)} %all_to_all.13), channel_id=1, replica_groups=mesh['grp'=4,'dev'=8] {'grp'}, use_global_device_ids=true, to_apply=%region_2.3 | all-reduce | flops 2304 | bytes 18432 | tf_op jit(solution)/shard_map/psum | solution.py:112
  90.0 11.3 %all_to_all.18 = f32[3,8,96]{2,0,1:T(4,128)S(1)} all-to-all(f32[3,8,96]{2,0,1:T(4,128)S(1)} %copy.28), channel_id=1, replica_groups=mesh['grp'=4,'dev'=8] {'dev'}, dimensions={1} | all-to-all | bytes 18432 | tf_op jit(solution)/shard_map/all_to_all | solution.py:113
  101.3 0.1 all_to_all.15
  101.4 0.6 copy-done.4
  102.0 1.0 fusion.41
  (40 shorter events, 0.8 us)
Async XLA Ops:
  0.0 0.8 copy-start.2
  1.9 24.1 %all-to-all-start = ((f32[6,8,96]{2,0,1:T(8,128)}), f32[6,8,96]{2,0,1:T(8,128)S(1)}, u32[]{:S(2)}, u32[]{:S(2)}) async-start(f32[6,8,96]{2,0,1:T(8,128)} %copy.24), calls=%async_computation | async-start | bytes 65536 | tf_op jit(solution)/shard_map/all_to_all | solution.py:83
  8.9 0.7 copy-start.7
  8.9 0.7 copy-start.6
  9.6 0.7 copy-start.3
  10.6 0.7 slice-start
  26.1 0.7 copy-start
  26.1 0.7 copy-start.1
  101.3 0.7 copy-start.4
  101.3 0.7 copy-start.5
where the time goes:
time: 104 us; the launch traced here: 103 us
  blocking collectives  76.7 us (74%)
  matrix products  9.42 us (9%)
  local copies, waits for them, and re-layouts  7.49 us (7%)
  starting transfers between devices  6.35 us (6%)
  other arithmetic  2.21 us (2%)
    psum x1, blocking collectives, body(): summed = lax.psum(partial_value, 'grp')  50.9 us
    all_gather x1, blocking collectives, body(): everything = lax.all_gather(source_pack, 'dev', axis=1, tiled=True)  14.5 us
    all_to_all x1, blocking collectives, body(): lax.all_to_all(summed, 'dev', split_axis=1, concat_axis=1, tiled=True)  11.3 us
    dot_general x2, matrix products, tile_irradiance(): jnp.einsum('bij,cbj->bci', factor, sources[7:10], precision=lax.Precision...  7.55 us
    all_to_all x1, starting transfers between devices, body(): lax.all_to_all(receiver_pack, 'dev', split_axis=1, concat_axis=1, tiled=T...  6.35 us
    unnamed x17, local copies, waits for them, and re-layouts  2.4 us
  transfers between devices with their start and end apart: 1, of which 0 were waited for; matrix products, arithmetic and copies ran while one was open for 1% of the time, Pallas kernels for 0%

commit v1 on v0

--- a/solution.py
+++ b/solution.py
@@ -80,7 +80,9 @@
         axis=0,
     )
     receiver_pack = jnp.concatenate([node_position, normals], axis=0)
-    linked = lax.all_to_all(receiver_pack, "dev", split_axis=1, concat_axis=1, tiled=True)
+    pieces = jnp.split(receiver_pack, lax.axis_size("dev"), axis=1)
+    arrived = lax.all_to_all(jnp.stack(pieces), "dev", 0, 0)
+    linked = jnp.concatenate(arrived, axis=1)
     receiver_tiles = linked.reshape(6, tile_count, TILE)
     everything = lax.all_gather(source_pack, "dev", axis=1, tiled=True)
     source_tiles = everything.reshape(10, -1, TILE)

time: 104 us -> 108 us (1.038)
  local copies, waits for them, and re-layouts: 7.49 us -> 10.7 us
    unnamed x17 -> x24, local copies, waits for them, and re-layouts: 2.4 us -> 6.89 us
    concatenate x5 -> x0, local copies, waits for them, and re-layouts: 1.64 us -> none  [body(): receiver_pack = jnp.concatenate([node_position, normals], axis=0)]
where the time goes in v1:
time: 108 us; the launch traced here: 107 us
  blocking collectives  76.7 us (71%)
  local copies, waits for them, and re-layouts  10.7 us (10%)
  matrix products  9.42 us (9%)
  starting transfers between devices  6.35 us (6%)
  other arithmetic  2.97 us (3%)
    psum x1, blocking collectives, body(): summed = lax.psum(partial_value, 'grp')  50.9 us
    all_gather x1, blocking collectives, body(): everything = lax.all_gather(source_pack, 'dev', axis=1, tiled=True)  14.5 us
    all_to_all x1, blocking collectives, body(): lax.all_to_all(summed, 'dev', split_axis=1, concat_axis=1, tiled=True)  11.3 us
    dot_general x2, matrix products, tile_irradiance(): jnp.einsum('bij,cbj->bci', factor, sources[7:10], precision=lax.Precision...  7.55 us
    unnamed x24, local copies, waits for them, and re-layouts  6.89 us
    all_to_all x1, starting transfers between devices, body(): arrived = lax.all_to_all(jnp.stack(pieces), 'dev', 0, 0)  6.35 us
  transfers between devices with their start and end apart: 1, of which 0 were waited for; matrix products, arithmetic and copies ran while one was open for 1% of the time, Pallas kernels for 0%

profile of v1, /device:TPU:0, one launch (start us, length us, event | category | flops | bytes accessed | tf_op | source)
XLA Modules:
  0.0 107.0 jit_solution(8497837663634550001)
XLA Ops:
  0.0 1.0 cosine_multiply_fusion
  1.0 0.6 constant_dynamic-update-slice_fusion.7
  1.6 0.7 constant_dynamic-update-slice_fusion.6
  2.2 0.7 constant_dynamic-update-slice_fusion.5
  2.9 0.7 constant_dynamic-update-slice_fusion.4
  3.6 0.6 constant_dynamic-update-slice_fusion.3
  4.2 0.7 constant_dynamic-update-slice_fusion.2
  4.8 0.7 constant_dynamic-update-slice_fusion.1
  5.5 0.7 constant_dynamic-update-slice_fusion
  6.1 6.4 %all-to-all-start = ((f32[8,6,96]{2,1,0:T(8,128)}), f32[8,6,96]{2,1,0:T(8,128)S(1)}, u32[]{:S(2)}, u32[]{:S(2)}) async-start(f32[8,6,96]{2,1,0:T(8,128)} %constant_dynamic-update-slice_fusion), calls=%async_computation | async-start | bytes 65536 | tf_op jit(solution)/shard_map/all_to_all | solution.py:84
  13.2 0.7 copy-done.7
  13.9 0.3 fusion.42
  14.1 0.4 copy-done.3
  14.6 0.3 convolution_divide_fusion
  14.8 0.4 slice-done
  15.3 14.5 %all_gather.3 = f32[10,2048]{1,0:T(8,128)S(1)} all-gather(f32[10,256]{1,0:T(8,128)S(1)} %fusion.48), channel_id=1, replica_groups=mesh['grp'=4,'dev'=8] {'dev'}, dimensions={1}, use_global_device_ids=true | all-gather | bytes 92160 | tf_op jit(solution)/shard_map/all_gather | solution.py:87
  30.0 0.6 copy-done.1
  30.7 12.4 %while.10 = (s32[]{:T(128)}, f32[3,6,128]{2,1,0:T(8,128)S(1)}, s32[]{:T(128)}, s32[128]{0:T(128)S(1)}, f32[10,16,128]{2,0,1:T(8,128)S(1)}, /*index=5*/s32[128]{0...) while((s32[]{:T(128)}, f32[3,6,128]{2,1,0:T(8,128)S(1)}, ...), condition=%wide.region_1.2_spmd, body=%wide.region_0.1_spmd.sunk | while | flops 17263236 | bytes 953843 | solution.py:112
  30.7 0.7 compare_and_fusion.5
  31.5 0.6 gather_fusion.1
  32.2 0.6 gather_fusion
  32.9 3.8 %convolution_multiply_fusion.2 = f32[16,3,128]{2,1,0:T(4,128)S(1)} fusion(f32[16,128]{1,0:T(8,128)S(1)} %bitcast.104, f32[16,128]{1,0:T(8,128)S(1)} %bitcast.105, f32[16,128]{1,0:T(8,128)S(1)} %bitcast.106, f32[16,128]{1,0:T(8,128)S(1)} %bitcast.111, f32[16,128]{1,0:T(8,128)S(1)} %bitcast.107, f32[16,128]{1,0:T(8,128)S(1)} %bitcast.112, ...), kind=kOutput, calls=%fused_computation.11.clone.1 | convolution fusion | flops 16783360 | bytes 164352 | tf_op jit(solution)/shard_map/while/body/bij,cbj->bci/dot_general | solution.py:44
  36.7 0.1 fusion.68
  36.8 0.7 compare_and_fusion.5
  37.7 0.6 gather_fusion.1
  38.4 0.6 gather_fusion
  39.1 3.8 %convolution_multiply_fusion.2 = f32[16,3,128]{2,1,0:T(4,128)S(1)} fusion(f32[16,128]{1,0:T(8,128)S(1)} %bitcast.104, f32[16,128]{1,0:T(8,128)S(1)} %bitcast.105, f32[16,128]{1,0:T(8,128)S(1)} %bitcast.106, f32[16,128]{1,0:T(8,128)S(1)} %bitcast.111, f32[16,128]{1,0:T(8,128)S(1)} %bitcast.107, f32[16,128]{1,0:T(8,128)S(1)} %bitcast.112, ...), kind=kOutput, calls=%fused_computation.11.clone.1 | convolution fusion | flops 16783360 | bytes 164352 | tf_op jit(solution)/shard_map/while/body/bij,cbj->bci/dot_general | solution.py:44
  42.9 0.1 fusion.68
  43.1 50.9 %psum.7 = f32[3,8,96]{2,1,0:T(8,128)S(1)} all-reduce(f32[3,8,96]{2,1,0:T(8,128)S(1)} %all_to_all.12), channel_id=1, replica_groups=mesh['grp'=4,'dev'=8] {'grp'}, use_global_device_ids=true, to_apply=%region_2.3 | all-reduce | flops 2304 | bytes 18432 | tf_op jit(solution)/shard_map/psum | solution.py:114
  94.0 11.3 %all_to_all.17 = f32[3,8,96]{2,0,1:T(4,128)S(1)} all-to-all(f32[3,8,96]{2,0,1:T(4,128)S(1)} %copy.26), channel_id=1, replica_groups=mesh['grp'=4,'dev'=8] {'dev'}, dimensions={1} | all-to-all | bytes 18432 | tf_op jit(solution)/shard_map/all_to_all | solution.py:115
  105.4 0.6 copy-done.4
  106.0 1.0 fusion.41
  (43 shorter events, 1.1 us)
Async XLA Ops:
  0.0 1.0 copy-start
  6.1 23.7 %all-to-all-start = ((f32[8,6,96]{2,1,0:T(8,128)}), f32[8,6,96]{2,1,0:T(8,128)S(1)}, u32[]{:S(2)}, u32[]{:S(2)}) async-start(f32[8,6,96]{2,1,0:T(8,128)} %constant_dynamic-update-slice_fusion), calls=%async_computation | async-start | bytes 65536 | tf_op jit(solution)/shard_map/all_to_all | solution.py:84
  13.2 0.7 copy-start.7
  13.2 0.7 copy-start.6
  13.9 0.7 copy-start.3
  14.6 0.7 slice-start
  30.0 0.7 copy-start.1
  30.0 0.7 copy-start.2
  105.3 0.7 copy-start.4
  105.3 0.7 copy-start.5

commit v2 on v0

--- a/solution.py
+++ b/solution.py
@@ -109,7 +109,8 @@
     batch_total = (live_count + step_slots - 1) // step_slots
     totals = lax.fori_loop(0, batch_total, add_batch, jnp.zeros((3, tile_count, TILE), jnp.float32))
     partial_value = totals.reshape(3, node_count)
-    summed = lax.psum(partial_value, "grp")
+    parts = lax.all_gather(partial_value, "grp")
+    summed = jnp.sum(parts, axis=0)
     irradiance = lax.all_to_all(summed, "dev", split_axis=1, concat_axis=1, tiled=True)
     pushed = jnp.dot(irradiance[:, leaf_count:], parent_onehot.T, precision=lax.Precision.HIGHEST)
     gathered = irradiance[:, :leaf_count] + pushed

time: 104 us -> 96.9 us (0.932)
  blocking collectives: 76.7 us -> 69.8 us
    psum x1 -> x0, blocking collectives: 50.9 us -> none  [body(): summed = lax.psum(partial_value, 'grp')]
    all_gather x0 -> x1, blocking collectives: none -> 45.4 us  [body(): parts = lax.all_gather(partial_value, 'grp')]
    all_to_all x1, blocking collectives: 11.3 us -> 9.97 us  [body(): lax.all_to_all(summed, 'dev', split_axis=1, concat_axis=1, tiled=True)]
where the time goes in v2:
time: 96.9 us; the launch traced here: 96.3 us
  blocking collectives  69.8 us (72%)
  matrix products  9.42 us (10%)
  local copies, waits for them, and re-layouts  7.51 us (8%)
  starting transfers between devices  6.35 us (7%)
  other arithmetic  2.22 us (2%)
    all_gather x1, blocking collectives, body(): parts = lax.all_gather(partial_value, 'grp')  45.4 us
    all_gather x1, blocking collectives, body(): everything = lax.all_gather(source_pack, 'dev', axis=1, tiled=True)  14.5 us
    all_to_all x1, blocking collectives, body(): lax.all_to_all(summed, 'dev', split_axis=1, concat_axis=1, tiled=True)  9.97 us
    dot_general x2, matrix products, tile_irradiance(): jnp.einsum('bij,cbj->bci', factor, sources[7:10], precision=lax.Precision...  7.55 us
    all_to_all x1, starting transfers between devices, body(): lax.all_to_all(receiver_pack, 'dev', split_axis=1, concat_axis=1, tiled=T...  6.35 us
    unnamed x17, local copies, waits for them, and re-layouts  2.4 us
  transfers between devices with their start and end apart: 1, of which 0 were waited for; matrix products, arithmetic and copies ran while one was open for 1% of the time, Pallas kernels for 0%

profile of v2, /device:TPU:0, one launch (start us, length us, event | category | flops | bytes accessed | tf_op | source)
XLA Modules:
  0.0 96.3 jit_solution(2491769508813459760)
XLA Ops:
  0.0 0.8 concatenate.17
  0.8 0.2 fusion.52
  1.2 0.6 copy.24
  1.9 6.4 %all-to-all-start = ((f32[6,8,96]{2,0,1:T(8,128)}), f32[6,8,96]{2,0,1:T(8,128)S(1)}, u32[]{:S(2)}, u32[]{:S(2)}) async-start(f32[6,8,96]{2,0,1:T(8,128)} %copy.24), calls=%async_computation | async-start | bytes 65536 | tf_op jit(solution)/shard_map/all_to_all | solution.py:83
  8.9 0.7 copy-done.7
  9.6 0.3 fusion.42
  9.9 0.4 copy-done.3
  10.3 0.3 convolution_divide_fusion
  10.6 0.7 slice-done
  11.3 14.5 %all_gather.6 = f32[10,2048]{1,0:T(8,128)S(1)} all-gather(f32[10,256]{1,0:T(8,128)S(1)} %fusion.48), channel_id=1, replica_groups=mesh['grp'=4,'dev'=8] {'dev'}, dimensions={1}, use_global_device_ids=true | all-gather | bytes 92160 | tf_op jit(solution)/shard_map/all_gather | solution.py:85
  26.1 0.6 copy-done
  26.7 12.4 %while.10 = (s32[]{:T(128)}, f32[3,6,128]{2,1,0:T(8,128)S(1)}, s32[]{:T(128)}, s32[128]{0:T(128)S(1)}, f32[10,16,128]{2,0,1:T(8,128)S(1)}, /*index=5*/s32[128]{0...) while((s32[]{:T(128)}, f32[3,6,128]{2,1,0:T(8,128)S(1)}, ...), condition=%wide.region_1.2_spmd, body=%wide.region_0.1_spmd.sunk | while | flops 17263236 | bytes 953843 | solution.py:110
  26.7 0.7 compare_and_fusion.5
  27.6 0.6 gather_fusion.1
  28.1 0.1 select_bitcast_fusion.5
  28.3 0.6 gather_fusion
  28.8 0.1 select_bitcast_fusion.4
  29.0 3.8 %convolution_multiply_fusion.2 = f32[16,3,128]{2,1,0:T(4,128)S(1)} fusion(f32[16,128]{1,0:T(8,128)S(1)} %bitcast.71, f32[16,128]{1,0:T(8,128)S(1)} %bitcast.72, f32[16,128]{1,0:T(8,128)S(1)} %bitcast.73, f32[16,128]{1,0:T(8,128)S(1)} %bitcast.78, f32[16,128]{1,0:T(8,128)S(1)} %bitcast.74, f32[16,128]{1,0:T(8,128)S(1)} %bitcast.79, ...), kind=kOutput, calls=%fused_computation.11.clone.1 | convolution fusion | flops 16783360 | bytes 164352 | tf_op jit(solution)/shard_map/while/body/bij,cbj->bci/dot_general | solution.py:44
  32.8 0.1 fusion.71
  32.9 0.7 compare_and_fusion.5
  33.7 0.6 gather_fusion.1
  34.3 0.1 select_bitcast_fusion.5
  34.5 0.6 gather_fusion
  35.0 0.1 select_bitcast_fusion.4
  35.2 3.8 %convolution_multiply_fusion.2 = f32[16,3,128]{2,1,0:T(4,128)S(1)} fusion(f32[16,128]{1,0:T(8,128)S(1)} %bitcast.71, f32[16,128]{1,0:T(8,128)S(1)} %bitcast.72, f32[16,128]{1,0:T(8,128)S(1)} %bitcast.73, f32[16,128]{1,0:T(8,128)S(1)} %bitcast.78, f32[16,128]{1,0:T(8,128)S(1)} %bitcast.74, f32[16,128]{1,0:T(8,128)S(1)} %bitcast.79, ...), kind=kOutput, calls=%fused_computation.11.clone.1 | convolution fusion | flops 16783360 | bytes 164352 | tf_op jit(solution)/shard_map/while/body/bij,cbj->bci/dot_general | solution.py:44
  38.9 0.1 fusion.71
  39.1 45.4 %all_gather.7 = f32[4,3,768]{2,1,0:T(4,128)S(1)} all-gather(f32[1,3,768]{2,1,0:T(4,128)S(1)} %all_gather_reshape.3), channel_id=1, replica_groups=mesh['grp'=4,'dev'=8] {'grp'}, dimensions={0}, use_global_device_ids=true | all-gather | bytes 46080 | tf_op jit(solution)/shard_map/all_gather | solution.py:112
  84.5 0.1 all_to_all.13
  84.6 10.0 %all_to_all.18 = f32[3,8,96]{2,0,1:T(4,128)S(1)} all-to-all(f32[3,8,96]{2,0,1:T(4,128)S(1)} %copy.28), channel_id=1, replica_groups=mesh['grp'=4,'dev'=8] {'dev'}, dimensions={1} | all-to-all | bytes 18432 | tf_op jit(solution)/shard_map/all_to_all | solution.py:114
  94.5 0.1 all_to_all.15
  94.6 0.6 copy-done.4
  95.3 1.0 %fusion.41 = f32[3,512]{1,0:T(4,128)} fusion(f32[3,512]{1,0:T(4,128)S(1)} %copy-done.4, f32[3,512]{1,0:T(4,128)S(1)} %copy-done.5, s32[512]{0:T(512)S(1)} %copy-done.7, f32[3,768]{1,0:T(4,128)S(1)} %all_to_all.15), kind=kOutput, calls=%fused_computation.63 | convolution fusion | flops 4854272 | bytes 29696 | tf_op jit(solution)/shard_map/dot_general | solution.py:115
  (42 shorter events, 0.9 us)
Async XLA Ops:
  0.0 0.8 copy-start.2
  1.9 24.1 %all-to-all-start = ((f32[6,8,96]{2,0,1:T(8,128)}), f32[6,8,96]{2,0,1:T(8,128)S(1)}, u32[]{:S(2)}, u32[]{:S(2)}) async-start(f32[6,8,96]{2,0,1:T(8,128)} %copy.24), calls=%async_computation | async-start | bytes 65536 | tf_op jit(solution)/shard_map/all_to_all | solution.py:83
  8.9 0.7 copy-start.7
  8.9 0.7 copy-start.6
  9.6 0.7 copy-start.3
  10.6 0.7 slice-start
  26.1 0.7 copy-start
  26.1 0.7 copy-start.1
  94.5 0.7 copy-start.4
  94.5 0.7 copy-start.5
